TPU v7x, 32 devices: a whole 2x2x4 slice. The times are simulated.
32 devices in a mesh: groups: 2 (over y), dp: 4 (over z), tensor: 4 (over x, core).
Axes of the slice: x: 2, y: 2, z: 4, core: 2. Of those that a mesh axis runs over, the one named last changes fastest.
Arguments:
- patches: bfloat16 [8192, 1280], P(('groups', 'dp')), parts along dimension 0, may hold values from -64 to 64
- grids: int32 [8, 2], P(('groups', 'dp')), parts along dimension 0, may hold values from 16 to 32, as said below
- dest: int32 [8, 256], P(('groups', 'dp')), parts along dimension 0, may hold values from 0 to 1535, as said below
- norm_gain: float32 [1280], replicated, may hold values from 0.1 to 1.9
- qkv_weight: bfloat16 [3, 1280, 1280], P(None, None, 'tensor'), may hold values from -8 to 8
- qkv_bias: float32 [3, 1280], P(None, 'tensor'), may hold values from -3 to 3
- proj_weight: bfloat16 [1280, 1280], P('tensor'), may hold values from -0.15625 to 0.15625
- proj_bias: float32 [1280], replicated, may hold values from -3 to 3
- merge_gain: float32 [1280], replicated, may hold values from 0.1 to 1.9
- w_first: bfloat16 [5120, 5120], P('dp', 'tensor'), may hold values from -0.078125 to 0.078125
- b_first: float32 [5120], P('tensor'), may hold values from -3 to 3
- w_second: bfloat16 [5120, 8192], P('tensor', 'dp'), may hold values from -0.078125 to 0.078125
- b_second: float32 [8192], P('tensor'), may hold values from -3 to 3
- text_embed: bfloat16 [3072, 8192], P(('groups', 'dp'), 'tensor'), parts along dimension 0, may hold values from -6 to 6
Outputs:
- sequence: bfloat16 [3072, 8192], P(('groups', 'dp'), 'tensor'), parts along dimension 0
There are 2 independent parts, one for each index of `groups`. A program takes and returns all parts, laid end to end along the dimension named above; an argument that names none is the same for every part. Nothing has to cross between parts.
Inputs may be any that keep to these rules, and one draw needn't show every extreme that they name: `grids`: both sides of every grid are even, at least 16 and at most 32; in each part along `groups`, the first image (the one on dp index 0) has the full 32 x 32 grid. The rows dest[i, j] with j < grids[i, 0] * grids[i, 1] / 4 are distinct over all images; the live rows of one image reach at most 64 rows in each aligned block of 384 sequence rows, and exactly that many for a full grid.
All inputs are finite; a program needn't handle non-finite values.
Results may differ from a plain program's by a relative error of at most 0.014.
Values may be sent and summed in bfloat16 or wider, within the bound.
A program may use at most 128 MiB of HBM per device.

v0:
```python
import math
import jax
import jax.numpy as jnp
from jax import lax
from jax.sharding import PartitionSpec as P

HEAD_DIM = 80
PATCHES = 1024
MERGED = 256


def rms_scale(values, gain):
    return values * lax.rsqrt(jnp.mean(values * values, axis=-1, keepdims=True) + 1e-06) * gain


def local(
    patches,
    grids,
    dest,
    norm_gain,
    qkv_weight,
    qkv_bias,
    proj_weight,
    proj_bias,
    merge_gain,
    w_first,
    b_first,
    w_second,
    b_second,
    text_embed,
):
    rows_dev = patches.shape[0]
    images_dev = grids.shape[0]
    heads_dev = qkv_weight.shape[2] // HEAD_DIM
    live_count = grids[:, 0] * grids[:, 1]
    normed = rms_scale(patches.astype(jnp.float32), norm_gain).astype(jnp.bfloat16)
    projected = (
        jnp.einsum("rv,jvc->jrc", normed, qkv_weight, preferred_element_type=jnp.float32)
        + qkv_bias[:, None, :]
    )
    projected = projected.astype(jnp.bfloat16).reshape(3, images_dev, PATCHES, heads_dev, HEAD_DIM)
    scores = jnp.einsum(
        "iqhd,ikhd->ihqk", projected[0], projected[1], preferred_element_type=jnp.float32
    ) / math.sqrt(HEAD_DIM)
    live_keys = jnp.arange(PATCHES, dtype=jnp.int32)[None, :] < live_count[:, None]
    scores = jnp.where(live_keys[:, None, None, :], scores, jnp.float32(-1e30))
    peak_score = jnp.max(scores, axis=-1, keepdims=True)
    exponent = jnp.exp(scores - peak_score)
    weights = (exponent / jnp.sum(exponent, axis=-1, keepdims=True)).astype(jnp.bfloat16)
    attended = jnp.einsum(
        "ihqk,ikhd->iqhd", weights, projected[2], preferred_element_type=jnp.float32
    )
    attended = attended.astype(jnp.bfloat16).reshape(rows_dev, heads_dev * HEAD_DIM)
    partial_value = jnp.dot(attended, proj_weight, preferred_element_type=jnp.float32).astype(
        jnp.bfloat16
    )
    summed = lax.psum(partial_value, "tensor").astype(jnp.float32)
    resid = patches.astype(jnp.float32) + summed + proj_bias
    merged_in = rms_scale(resid, merge_gain).astype(jnp.bfloat16)
    merged_in = merged_in.reshape(rows_dev // 4, 4 * patches.shape[1])
    merged_dev = merged_in.shape[0]
    received = lax.all_to_all(merged_in, "dp", split_axis=1, concat_axis=0, tiled=True)
    first_out = lax.psum_scatter(
        jnp.dot(received, w_first, preferred_element_type=jnp.float32).astype(jnp.bfloat16),
        "dp",
        scatter_dimension=0,
        tiled=True,
    ).astype(jnp.float32)
    hidden = jax.nn.gelu(first_out + b_first, approximate=False).astype(jnp.bfloat16)
    second_rows = jnp.dot(
        hidden,
        lax.all_gather(w_second, "dp", axis=1, tiled=True),
        preferred_element_type=jnp.float32,
    ).astype(jnp.bfloat16)
    visual = lax.psum_scatter(second_rows, "tensor", scatter_dimension=1, tiled=True).astype(
        jnp.float32
    )
    visual = (visual + b_second).astype(jnp.bfloat16)
    feature_count = visual.shape[1]
    dp_count = lax.axis_size("dp")
    seq_rows = text_embed.shape[0]
    capacity = images_dev * (MERGED // dp_count)
    live_rows = (jnp.arange(MERGED, dtype=jnp.int32)[None, :] < (live_count // 4)[:, None]).reshape(
        merged_dev
    )
    dest_flat = dest.reshape(merged_dev)
    shard_id = jnp.where(live_rows, dest_flat // seq_rows, dp_count)
    local_row = dest_flat % seq_rows
    one_hot = (shard_id[:, None] == jnp.arange(dp_count, dtype=jnp.int32)[None, :]).astype(
        jnp.int32
    )
    before = jnp.cumsum(one_hot, axis=0) - one_hot
    slot_index = jnp.sum(before * one_hot, axis=1)
    buffer = (
        jnp.zeros((dp_count, capacity, feature_count), jnp.bfloat16)
        .at[shard_id, slot_index]
        .set(visual, mode="drop")
    )
    positions = (
        jnp.full((dp_count, capacity), seq_rows, jnp.int32)
        .at[shard_id, slot_index]
        .set(local_row, mode="drop")
    )
    arrived, arrived_rows = (
        lax.all_to_all(buffer, "dp", split_axis=0, concat_axis=0, tiled=True),
        lax.all_to_all(positions, "dp", split_axis=0, concat_axis=0, tiled=True),
    )
    sequence = text_embed.at[arrived_rows.reshape(-1)].set(
        arrived.reshape(-1, feature_count), mode="drop"
    )
    return sequence


def solution(mesh):
    in_specs = (
        P(("groups", "dp"), None),
        P(("groups", "dp"), None),
        P(("groups", "dp"), None),
        P(),
        P(None, None, "tensor"),
        P(None, "tensor"),
        P("tensor", None),
        P(),
        P(),
        P("dp", "tensor"),
        P("tensor"),
        P("tensor", "dp"),
        P("tensor"),
        P(("groups", "dp"), "tensor"),
    )
    out_specs = P(("groups", "dp"), "tensor")
    return jax.shard_map(local, mesh=mesh, in_specs=in_specs, out_specs=out_specs, check_vma=False)
```

profile of v0, /device:TPU:0, one launch (start us, length us, event | category | flops | bytes accessed | tf_op | source)
XLA Modules:
  0.0 749.1 jit_solution(11529100986900097305)
XLA Ops:
  6.5 2.9 copy.35
  13.1 2.9 fusion.15
  15.9 1.3 fusion.103
  17.3 10.9 %fusion.105 = (f32[4,1024]{1,0:T(4,128)S(1)}, f32[4,1024,1024]{1,2,0:T(8,128)}) fusion(pred[1024]{0:T(1024)(128)(4,1)S(1)} %iota_compare_fusion, bf16[1024,4,80]{0,2,1:T(8,128)(2,1)} %bitcast.76, bf16[1024,4,80]{0,2,1:T(8,128)(2,1)} %bitcast.75), kind=kOutput, calls=%fused_computation.150 | convolution fusion | flops 687866880 | bytes 18105344 | tf_op jit(solution)/shard_map/sub | solution.py:48
  28.1 7.6 %fusion.20 = bf16[4,80,1024]{2,1,0:T(8,128)(2,1)S(1)} fusion(bf16[1024,4,80]{0,2,1:T(8,128)(2,1)} %bitcast.74, f32[4,1024,1024]{1,2,0:T(8,128)} %get-tuple-element.17, f32[4,1024]{1,0:T(4,128)S(1)} %get-tuple-element.16), kind=kOutput, calls=%fused_computation.33 | convolution fusion | flops 679804928 | bytes 18104320 | tf_op jit(solution)/shard_map/ihqk,ikhd->iqhd/dot_general | solution.py:50
  35.8 3.1 convolution_convert_fusion.2
  39.1 62.5 %all-reduce.2.cloned.1.call-done = bf16[1024,1280]{1,0:T(8,128)(2,1)} async-done(((bf16[1024,1280]{1,0:T(8,128)(2,1)}), bf16[1024,1280]{1,0:T(8,128)(2,1)}) %all-reduce.2.cloned.1.call-update) | async-done | bytes 2621456 | tf_op jit(solution)/shard_map/psum | solution.py:57
  101.7 3.8 multiply_reduce_fusion
  105.8 2.6 multiply_convert_fusion
  108.4 5.6 all_to_all.25
  114.0 2.1 copy.26
  116.0 63.6 %all_to_all.33 = bf16[256,4,1280]{2,0,1:T(8,128)(2,1)S(1)} all-to-all(bf16[256,4,1280]{2,0,1:T(8,128)(2,1)S(1)} %copy.26), channel_id=1, replica_groups=mesh['groups'=2,'dp'=4,'tensor'=4] {'dp'}, dimensions={1} | all-to-all | bytes 5242880 | tf_op jit(solution)/shard_map/all_to_all | solution.py:62
  179.6 4.9 convolution_convert_fusion.1
  185.3 50.0 %reduce-scatter.3.cloned.1.call-done = bf16[256,1280]{1,0:T(8,128)(2,1)} async-done(((bf16[1024,1280]{1,0:T(8,128)(2,1)}), bf16[256,1280]{1,0:T(8,128)(2,1)}) %reduce-scatter.3.cloned.1.call-update) | async-done | bytes 655376 | tf_op jit(solution)/shard_map/reduce_scatter | solution.py:63
  235.3 358.0 %all-gather.2.cloned.1.call-done = bf16[1280,8192]{1,0:T(8,128)(2,1)} async-done(((bf16[1280,2048]{1,0:T(8,128)(2,1)}), bf16[1280,8192]{1,0:T(8,128)(2,1)}) %all-gather.2.cloned.1.call-update) | async-done | bytes 20971536 | tf_op jit(solution)/shard_map/all_gather | solution.py:72
  593.3 17.4 %convolution_convert_fusion = bf16[256,8192]{1,0:T(8,128)(2,1)} fusion(bf16[1280,8192]{1,0:T(8,128)(2,1)} %all-gather.2.cloned.1.call-done, bf16[256,1280]{1,0:T(8,128)(2,1)} %reduce-scatter.3.cloned.1.call-done, f32[1280]{0:T(1024)S(1)} %copy-done.13), kind=kOutput, calls=%fused_computation.8 | convolution fusion | flops 5392760832 | bytes 25826304 | tf_op jit(solution)/shard_map/dot_general | solution.py:70
  611.4 1.2 reduce-window.6
  613.7 38.8 %scatter_fusion = s32[4,64]{1,0:T(4,128)} fusion(s32[4,64]{1,0:T(4,128)} %broadcast_in_dim.23, s32[256]{0:T(256)S(1)} %bitcast.71, s32[256]{0:T(256)S(1)} %get-tuple-element.10), kind=kCustom, calls=%fused_computation | custom fusion | bytes 5120 | tf_op jit(solution)/shard_map/scatter | solution.py:102
  652.5 3.2 all-to-all-start
  655.7 1.5 add_convert_fusion.1
  658.4 48.1 %scatter_fusion.1 = bf16[4,64,2048]{2,1,0:T(8,128)(2,1)} fusion(bf16[4,64,2048]{2,1,0:T(8,128)(2,1)} %broadcast_in_dim.28, s32[256]{0:T(256)S(1)} %bitcast.72, bf16[256,2048]{1,0:T(8,128)(2,1)S(1)} %add_convert_fusion.1), kind=kCustom, calls=%fused_computation.1 | custom fusion | bytes 3147776 | tf_op jit(solution)/shard_map/scatter | solution.py:97
  706.5 5.0 all-to-all-start.2
  712.8 24.2 %all-to-all-done.2 = bf16[4,64,2048]{2,1,0:T(8,128)(2,1)} async-done(((bf16[4,64,2048]{2,1,0:T(8,128)(2,1)}), bf16[4,64,2048]{2,1,0:T(8,128)(2,1)}, u32[]{:S(2)}, u32[]{:S(2)}) %all-to-all-start.2) | async-done | bytes 1048608 | tf_op jit(solution)/shard_map/all_to_all | solution.py:105
  736.9 5.7 scatter_fusion.2
  (64 shorter events, 7.8 us)
Async XLA Ops:
  6.5 173.1 %copy-start = (bf16[1280,1280]{1,0:T(8,128)(2,1)S(1)}, bf16[1280,1280]{1,0:T(8,128)(2,1)}, u32[]{:S(2)}) copy-start(bf16[1280,1280]{1,0:T(8,128)(2,1)} %param.23) | copy-start | bytes 9830404
  6.5 2.9 copy-start.9
  6.5 95.1 %all-reduce.2.cloned.1.call-start = ((), (), s32[]{:S(2)}) async-start(), calls=%async_computation.5 | async-start | bytes 5242880 | tf_op jit(solution)/shard_map/psum | solution.py:57
  6.5 4.8 copy-start.2
  11.4 1.7 copy-start.10
  11.4 1.7 copy-start.12
  11.4 1.7 copy-start.14
  28.1 7.6 %copy-start.11 = (bf16[320,1280]{1,0:T(8,128)(2,1)S(1)}, bf16[320,1280]{1,0:T(8,128)(2,1)}, u32[]{:S(2)}) copy-start(bf16[320,1280]{1,0:T(8,128)(2,1)} %param.20) | copy-start | bytes 2457604
  38.9 62.8 %copy-start.5 = (f32[1280]{0:T(1024)S(1)}, f32[1280]{0:T(1024)}, u32[]{:S(2)}) copy-start(f32[1280]{0:T(1024)} %param.21) | copy-start | bytes 15364
  38.9 66.6 %copy-start.7 = (f32[1280]{0:T(1024)S(1)}, f32[1280]{0:T(1024)}, u32[]{:S(2)}) copy-start(f32[1280]{0:T(1024)} %param.22) | copy-start | bytes 15364
  38.9 196.4 %reduce-scatter.3.cloned.1.call-start = ((), (), s32[]{:S(2)}) async-start(), calls=%async_computation.6 | async-start | bytes 3276800 | tf_op jit(solution)/shard_map/reduce_scatter | solution.py:63
  101.7 3.8 copy-start.3
  101.7 4.1 copy-start.4
  184.5 408.8 %copy-start.13 = (f32[1280]{0:T(1024)S(1)}, f32[1280]{0:T(1024)}, u32[]{:S(2)}) copy-start(f32[1280]{0:T(1024)} %param.24) | copy-start | bytes 15364
  184.5 408.8 %all-gather.2.cloned.1.call-start = ((), (), s32[]{:S(2)}) async-start(), calls=%async_computation.7 | async-start | bytes 26214400 | tf_op jit(solution)/shard_map/all_gather | solution.py:72
  185.2 470.5 %reduce-scatter.5.cloned.1.call-start = ((), (), s32[]{:S(2)}) async-start(), calls=%async_computation.8 | async-start | bytes 5242880 | tf_op jit(solution)/shard_map/reduce_scatter | solution.py:75
  610.7 0.7 copy-start.6
  610.7 45.0 %copy-start.8 = (f32[2048]{0:T(1024)S(1)}, f32[2048]{0:T(1024)}, u32[]{:S(2)}) copy-start(f32[2048]{0:T(1024)} %param.26) | copy-start | bytes 24580
  652.5 54.0 %all-to-all-start = ((s32[4,1,64]{2,1,0:T(1,128)}), s32[4,1,64]{2,1,0:T(1,128)S(1)}, u32[]{:S(2)}, u32[]{:S(2)}) async-start(s32[4,1,64]{2,1,0:T(1,128)} %bitcast.12), calls=%async_computation | async-start | bytes 4096 | tf_op jit(solution)/shard_map/all_to_all | solution.py:106
  706.5 30.4 %all-to-all-start.2 = ((bf16[4,64,2048]{2,1,0:T(8,128)(2,1)}), bf16[4,64,2048]{2,1,0:T(8,128)(2,1)}, u32[]{:S(2)}, u32[]{:S(2)}) async-start(bf16[4,64,2048]{2,1,0:T(8,128)(2,1)} %scatter_fusion.1), calls=%async_computation.4 | async-start | bytes 2097152 | tf_op jit(solution)/shard_map/all_to_all | solution.py:105
  736.9 5.7 copy-start.1
Sparse Core Ops, SparseCore 0:
  39.0 62.6 all-reduce.1
  184.6 50.6 reduce-scatter.2
  236.9 356.3 all-gather.1
  610.8 42.9 reduce-scatter.4
where the time goes:
time: 753 us; the launch traced here: 749 us
  waiting for transfers between devices  495 us (66%)
  local copies, waits for them, and re-layouts  110 us (15%)
  blocking collectives  63.6 us (8%)
  matrix products  46.7 us (6%)
  between operations  14.6 us (2%)
  other arithmetic  10.6 us (1%)
  starting transfers between devices  8.51 us (1%)
    all_gather x1, waiting for transfers between devices, local(): lax.all_gather(w_second, 'dp', axis=1, tiled=True)  358 us
    all_to_all x1, blocking collectives, local(): lax.all_to_all(merged_in, 'dp', split_axis=1, concat_axis=0, tiled=True)  63.6 us
    psum x1, waiting for transfers between devices, local(): summed = lax.psum(partial_value, 'tensor').astype(jnp.float32)  62.5 us
    reduce_scatter x1, waiting for transfers between devices, local(): lax.psum_scatter(jnp.dot(received, w_first, preferred_element_type=jnp.fl...  50 us
    scatter x1, local copies, waits for them, and re-layouts, local(): buffer = jnp.zeros((dp_count, capacity, feature_count), jnp.bfloat16).at[...  48.1 us
    scatter x1, local copies, waits for them, and re-layouts, local(): positions = jnp.full((dp_count, capacity), seq_rows, jnp.int32).at[shard_...  38.8 us
    all_to_all x1, waiting for transfers between devices, local(): lax.all_to_all(buffer, 'dp', split_axis=0, concat_axis=0, tiled=True)  24.2 us
    dot_general x1, matrix products, local(): jnp.dot(hidden, lax.all_gather(w_second, 'dp', axis=1, tiled=True), prefe...  17.4 us
  transfers between devices with their start and end apart: 6, of which 4 were waited for; matrix products, arithmetic and copies ran while one was open for 12% of the time, Pallas kernels for 0%

commit v1 on v0

--- a/solution.py
+++ b/solution.py
@@ -59,7 +59,10 @@
     merged_in = rms_scale(resid, merge_gain).astype(jnp.bfloat16)
     merged_in = merged_in.reshape(rows_dev // 4, 4 * patches.shape[1])
     merged_dev = merged_in.shape[0]
-    received = lax.all_to_all(merged_in, "dp", split_axis=1, concat_axis=0, tiled=True)
+    received = jnp.concatenate(
+        lax.all_to_all(jnp.stack(jnp.split(merged_in, lax.axis_size("dp"), axis=1)), "dp", 0, 0),
+        axis=0,
+    )
     first_out = lax.psum_scatter(
         jnp.dot(received, w_first, preferred_element_type=jnp.float32).astype(jnp.bfloat16),
         "dp",

time: 753 us -> 751 us (level)
    all_to_all x2 -> x0, local copies, waits for them, and re-layouts: 7.62 us -> none  [local(): lax.all_to_all(merged_in, 'dp', split_axis=1, concat_axis=0, tiled=True)]
where the time goes in v1:
time: 751 us; the launch traced here: 748 us
  waiting for transfers between devices  495 us (66%)
  local copies, waits for them, and re-layouts  108 us (14%)
  blocking collectives  63.6 us (8%)
  matrix products  46.7 us (6%)
  between operations  14.7 us (2%)
  other arithmetic  10.9 us (1%)
  starting transfers between devices  8.51 us (1%)
    all_gather x1, waiting for transfers between devices, local(): lax.all_gather(w_second, 'dp', axis=1, tiled=True)  358 us
    all_to_all x1, blocking collectives, local(): lax.all_to_all(jnp.stack(jnp.split(merged_in, lax.axis_size('dp'), axis=1...  63.6 us
    psum x1, waiting for transfers between devices, local(): summed = lax.psum(partial_value, 'tensor').astype(jnp.float32)  62.6 us
    reduce_scatter x1, waiting for transfers between devices, local(): lax.psum_scatter(jnp.dot(received, w_first, preferred_element_type=jnp.fl...  50 us
    scatter x1, local copies, waits for them, and re-layouts, local(): buffer = jnp.zeros((dp_count, capacity, feature_count), jnp.bfloat16).at[...  48.1 us
    scatter x1, local copies, waits for them, and re-layouts, local(): positions = jnp.full((dp_count, capacity), seq_rows, jnp.int32).at[shard_...  38.8 us
    all_to_all x1, waiting for transfers between devices, local(): lax.all_to_all(buffer, 'dp', split_axis=0, concat_axis=0, tiled=True)  24.2 us
    dot_general x1, matrix products, local(): jnp.dot(hidden, lax.all_gather(w_second, 'dp', axis=1, tiled=True), prefe...  17.4 us
  transfers between devices with their start and end apart: 6, of which 4 were waited for; matrix products, arithmetic and copies ran while one was open for 12% of the time, Pallas kernels for 0%

profile of v1, /device:TPU:0, one launch (start us, length us, event | category | flops | bytes accessed | tf_op | source)
XLA Modules:
  0.0 748.0 jit_solution(11138553657485548527)
XLA Ops:
  6.5 2.9 copy.30
  12.1 2.9 fusion.15
  15.0 1.3 fusion.103
  16.3 10.9 %fusion.105 = (f32[4,1024]{1,0:T(4,128)S(1)}, f32[4,1024,1024]{1,2,0:T(8,128)}) fusion(pred[1024]{0:T(1024)(128)(4,1)S(1)} %iota_compare_fusion, bf16[1024,4,80]{0,2,1:T(8,128)(2,1)} %bitcast.82, bf16[1024,4,80]{0,2,1:T(8,128)(2,1)} %bitcast.81), kind=kOutput, calls=%fused_computation.155 | convolution fusion | flops 687866880 | bytes 18105344 | tf_op jit(solution)/shard_map/sub | solution.py:48
  27.2 7.6 %fusion.20 = bf16[4,80,1024]{2,1,0:T(8,128)(2,1)S(1)} fusion(bf16[1024,4,80]{0,2,1:T(8,128)(2,1)} %bitcast.80, f32[4,1024,1024]{1,2,0:T(8,128)} %get-tuple-element.21, f32[4,1024]{1,0:T(4,128)S(1)} %get-tuple-element.20), kind=kOutput, calls=%fused_computation.34 | convolution fusion | flops 679804928 | bytes 18104320 | tf_op jit(solution)/shard_map/ihqk,ikhd->iqhd/dot_general | solution.py:50
  34.8 3.1 convolution_convert_fusion.2
  38.2 62.6 %all-reduce.2.cloned.1.call-done = bf16[1024,1280]{1,0:T(8,128)(2,1)} async-done(((bf16[1024,1280]{1,0:T(8,128)(2,1)}), bf16[1024,1280]{1,0:T(8,128)(2,1)}) %all-reduce.2.cloned.1.call-update) | async-done | bytes 2621456 | tf_op jit(solution)/shard_map/psum | solution.py:57
  100.7 3.8 multiply_reduce_fusion
  104.8 2.6 multiply_convert_fusion
  107.4 5.2 reshape.270
  112.7 1.9 slice_bitcast_fusion.3
  114.9 63.6 %all_to_all.19 = bf16[4,256,1280]{2,1,0:T(8,128)(2,1)S(1)} all-to-all(bf16[4,256,1280]{2,1,0:T(8,128)(2,1)S(1)} %pad_maximum_fusion), channel_id=1, replica_groups=mesh['groups'=2,'dp'=4,'tensor'=4] {'dp'}, dimensions={0} | all-to-all | bytes 5242880 | tf_op jit(solution)/shard_map/all_to_all | solution.py:63
  178.4 4.9 convolution_convert_fusion.1
  184.1 50.0 %reduce-scatter.3.cloned.1.call-done = bf16[256,1280]{1,0:T(8,128)(2,1)} async-done(((bf16[1024,1280]{1,0:T(8,128)(2,1)}), bf16[256,1280]{1,0:T(8,128)(2,1)}) %reduce-scatter.3.cloned.1.call-update) | async-done | bytes 655376 | tf_op jit(solution)/shard_map/reduce_scatter | solution.py:66
  234.1 358.0 %all-gather.2.cloned.1.call-done = bf16[1280,8192]{1,0:T(8,128)(2,1)} async-done(((bf16[1280,2048]{1,0:T(8,128)(2,1)}), bf16[1280,8192]{1,0:T(8,128)(2,1)}) %all-gather.2.cloned.1.call-update) | async-done | bytes 20971536 | tf_op jit(solution)/shard_map/all_gather | solution.py:75
  592.2 17.4 %convolution_convert_fusion = bf16[256,8192]{1,0:T(8,128)(2,1)} fusion(bf16[1280,8192]{1,0:T(8,128)(2,1)} %all-gather.2.cloned.1.call-done, bf16[256,1280]{1,0:T(8,128)(2,1)} %reduce-scatter.3.cloned.1.call-done, f32[1280]{0:T(1024)S(1)} %copy-done.13), kind=kOutput, calls=%fused_computation.8 | convolution fusion | flops 5392760832 | bytes 25826304 | tf_op jit(solution)/shard_map/dot_general | solution.py:73
  610.3 1.2 reduce-window.6
  612.5 38.8 %scatter_fusion = s32[4,64]{1,0:T(4,128)} fusion(s32[4,64]{1,0:T(4,128)} %broadcast_in_dim.23, s32[256]{0:T(256)S(1)} %bitcast.77, s32[256]{0:T(256)S(1)} %get-tuple-element.14), kind=kCustom, calls=%fused_computation | custom fusion | bytes 5120 | tf_op jit(solution)/shard_map/scatter | solution.py:105
  651.3 3.2 all-to-all-start
  654.6 1.5 add_convert_fusion.1
  657.2 48.1 %scatter_fusion.1 = bf16[4,64,2048]{2,1,0:T(8,128)(2,1)} fusion(bf16[4,64,2048]{2,1,0:T(8,128)(2,1)} %broadcast_in_dim.28, s32[256]{0:T(256)S(1)} %bitcast.78, bf16[256,2048]{1,0:T(8,128)(2,1)S(1)} %add_convert_fusion.1), kind=kCustom, calls=%fused_computation.1 | custom fusion | bytes 3147776 | tf_op jit(solution)/shard_map/scatter | solution.py:100
  705.3 5.0 all-to-all-start.2
  711.6 24.2 %all-to-all-done.2 = bf16[4,64,2048]{2,1,0:T(8,128)(2,1)} async-done(((bf16[4,64,2048]{2,1,0:T(8,128)(2,1)}), bf16[4,64,2048]{2,1,0:T(8,128)(2,1)}, u32[]{:S(2)}, u32[]{:S(2)}) %all-to-all-start.2) | async-done | bytes 1048608 | tf_op jit(solution)/shard_map/all_to_all | solution.py:108
  735.8 5.7 scatter_fusion.2
  (65 shorter events, 7.1 us)
Async XLA Ops:
  6.5 171.9 %copy-start = (bf16[1280,1280]{1,0:T(8,128)(2,1)S(1)}, bf16[1280,1280]{1,0:T(8,128)(2,1)}, u32[]{:S(2)}) copy-start(bf16[1280,1280]{1,0:T(8,128)(2,1)} %param.23) | copy-start | bytes 9830404
  6.5 2.9 copy-start.9
  6.5 94.2 %all-reduce.2.cloned.1.call-start = ((), (), s32[]{:S(2)}) async-start(), calls=%async_computation.5 | async-start | bytes 5242880 | tf_op jit(solution)/shard_map/psum | solution.py:57
  6.5 4.9 copy-start.2
  9.4 2.6 copy-start.10
  9.4 2.7 copy-start.12
  9.4 2.7 copy-start.14
  27.2 7.6 %copy-start.11 = (bf16[320,1280]{1,0:T(8,128)(2,1)S(1)}, bf16[320,1280]{1,0:T(8,128)(2,1)}, u32[]{:S(2)}) copy-start(bf16[320,1280]{1,0:T(8,128)(2,1)} %param.20) | copy-start | bytes 2457604
  37.9 62.8 %copy-start.5 = (f32[1280]{0:T(1024)S(1)}, f32[1280]{0:T(1024)}, u32[]{:S(2)}) copy-start(f32[1280]{0:T(1024)} %param.21) | copy-start | bytes 15364
  37.9 66.6 %copy-start.7 = (f32[1280]{0:T(1024)S(1)}, f32[1280]{0:T(1024)}, u32[]{:S(2)}) copy-start(f32[1280]{0:T(1024)} %param.22) | copy-start | bytes 15364
  37.9 196.2 %reduce-scatter.3.cloned.1.call-start = ((), (), s32[]{:S(2)}) async-start(), calls=%async_computation.6 | async-start | bytes 3276800 | tf_op jit(solution)/shard_map/reduce_scatter | solution.py:66
  100.7 3.8 copy-start.3
  100.7 4.1 copy-start.4
  183.3 408.8 %copy-start.13 = (f32[1280]{0:T(1024)S(1)}, f32[1280]{0:T(1024)}, u32[]{:S(2)}) copy-start(f32[1280]{0:T(1024)} %param.24) | copy-start | bytes 15364
  183.3 408.8 %all-gather.2.cloned.1.call-start = ((), (), s32[]{:S(2)}) async-start(), calls=%async_computation.7 | async-start | bytes 26214400 | tf_op jit(solution)/shard_map/all_gather | solution.py:75
  184.1 470.5 %reduce-scatter.5.cloned.1.call-start = ((), (), s32[]{:S(2)}) async-start(), calls=%async_computation.8 | async-start | bytes 5242880 | tf_op jit(solution)/shard_map/reduce_scatter | solution.py:78
  609.5 0.7 copy-start.6
  609.6 45.0 %copy-start.8 = (f32[2048]{0:T(1024)S(1)}, f32[2048]{0:T(1024)}, u32[]{:S(2)}) copy-start(f32[2048]{0:T(1024)} %param.26) | copy-start | bytes 24580
  651.3 54.0 %all-to-all-start = ((s32[4,1,64]{2,1,0:T(1,128)}), s32[4,1,64]{2,1,0:T(1,128)S(1)}, u32[]{:S(2)}, u32[]{:S(2)}) async-start(s32[4,1,64]{2,1,0:T(1,128)} %bitcast.12), calls=%async_computation | async-start | bytes 4096 | tf_op jit(solution)/shard_map/all_to_all | solution.py:109
  705.3 30.4 %all-to-all-start.2 = ((bf16[4,64,2048]{2,1,0:T(8,128)(2,1)}), bf16[4,64,2048]{2,1,0:T(8,128)(2,1)}, u32[]{:S(2)}, u32[]{:S(2)}) async-start(bf16[4,64,2048]{2,1,0:T(8,128)(2,1)} %scatter_fusion.1), calls=%async_computation.4 | async-start | bytes 2097152 | tf_op jit(solution)/shard_map/all_to_all | solution.py:108
  735.8 5.7 copy-start.1
Sparse Core Ops, SparseCore 0:
  38.0 62.6 all-reduce.1
  183.4 50.6 reduce-scatter.2
  235.7 356.3 all-gather.1
  609.7 42.9 reduce-scatter.4
